TPU v7x, 32 devices: a 4x4x1 block of a 4x4x8 slice. The times are simulated.
32 devices in a mesh: videos: 1 (over z), frames: 32 (over y, x, core).
Axes of the slice: x: 4, y: 4, z: 1, core: 2. Of those that a mesh axis runs over, the one named last changes fastest.
The devices are a block of a 4x4x8 slice.
Arguments:
- latents: float32 [128, 256, 4], P(('videos', 'frames'))
- slot_mod: float32 [128, 6, 6, 384], P(('videos', 'frames'))
- step_dt: float32 [128], P(('videos', 'frames'))
- new_noise: float32 [4, 256, 4], P('videos')
- w_in: bfloat16 [4, 384], replicated
- spat_qkv: bfloat16 [6, 3, 384, 6, 64], replicated
- spat_out: bfloat16 [6, 6, 64, 384], replicated
- temp_qkv: bfloat16 [6, 3, 384, 6, 64], replicated
- temp_out: bfloat16 [6, 6, 64, 384], replicated
- temp_bias: float32 [6, 6, 9], replicated
- w_up: bfloat16 [6, 384, 1536], replicated
- w_down: bfloat16 [6, 1536, 384], replicated
- w_out: bfloat16 [384, 4], replicated
Outputs:
- output 1: float32 [4, 256, 4], P('videos', 'frames')
- output 2: float32 [128, 256, 4], P(('videos', 'frames'))
All inputs are finite; a program needn't handle non-finite values.
Results may differ from a plain program's by a relative error of at most 0.0064095.
Values are sent between devices in bfloat16 or wider.
A program may use at most 768 MiB of HBM per device.

v0:
```python
import jax
import jax.numpy as jnp
from jax import lax
from jax.sharding import PartitionSpec as P

NORM_EPS = 1e-6


def modulate(x, shift, scale):
    centred = x - jnp.mean(x, axis=-1, keepdims=True)
    variance = jnp.mean(jnp.square(centred), axis=-1, keepdims=True)
    normed = centred * lax.rsqrt(variance + NORM_EPS)
    return (normed * (1.0 + scale[:, None, :]) + shift[:, None, :]).astype(jnp.bfloat16)


def spatial_block(x, shift, scale, w_qkv, w_proj):
    u = modulate(x, shift, scale)
    heads_qkv = jnp.einsum('fpd,jdhe->jfphe', u, w_qkv, preferred_element_type=jnp.float32).astype(jnp.bfloat16)
    scores = jnp.einsum('fqhe,fkhe->fhqk', heads_qkv[0], heads_qkv[1], preferred_element_type=jnp.float32)
    prob_mat = jax.nn.softmax(scores * w_qkv.shape[-1] ** -0.5, axis=-1).astype(jnp.bfloat16)
    attended = jnp.einsum('fhqk,fkhe->fqhe', prob_mat, heads_qkv[2], preferred_element_type=jnp.float32).astype(jnp.bfloat16)
    return x + jnp.einsum('fphe,hed->fpd', attended, w_proj, preferred_element_type=jnp.float32)


def mlp_block(x, shift, scale, up_l, down_l):
    u = modulate(x, shift, scale)
    hidden = jax.nn.gelu(jnp.einsum('fpd,dm->fpm', u, up_l, preferred_element_type=jnp.float32), approximate=True).astype(jnp.bfloat16)
    return x + jnp.einsum('fpm,md->fpd', hidden, down_l, preferred_element_type=jnp.float32)


def temporal_attend(queries, key_side, value_side, rel_table, first_slots, low_slot, high_slot):
    q_count = queries.shape[1]
    k_span = key_side.shape[1]
    radius = (rel_table.shape[-1] - 1) // 2
    k_pos = jnp.arange(k_span) - radius
    offset = k_pos[None, :] - jnp.arange(q_count)[:, None]
    rel_bias = rel_table[:, jnp.clip(offset + radius, 0, 2 * radius)]
    k_slot = first_slots[:, None] + k_pos[None, :]
    allowed = (jnp.abs(offset) <= radius)[None] & ((k_slot >= low_slot) & (k_slot < high_slot))[:, None, :]
    scores = jnp.einsum('gaphe,gbphe->gphab', queries, key_side, preferred_element_type=jnp.float32)
    scores = scores * queries.shape[-1] ** -0.5 + rel_bias[None, None]
    scores = jnp.where(allowed[:, None, None], scores, -1e30)
    prob_mat = jax.nn.softmax(scores, axis=-1).astype(jnp.bfloat16)
    return jnp.einsum('gphab,gbphe->gaphe', prob_mat, value_side, preferred_element_type=jnp.float32).astype(jnp.bfloat16)


def solution(mesh):
    groups = mesh.shape['frames']
    right_pairs = [(source, source + 1) for source in range(groups - 1)]
    left_pairs = [(source + 1, source) for source in range(groups - 1)]
    slot_spec = P(('videos', 'frames'))

    def per_device(latents, slot_mod, step_dt, new_noise, w_in, spat_qkv, spat_out, temp_qkv, temp_out, temp_bias, w_up, w_down, w_out):
        per_dev = latents.shape[0]
        layers = spat_qkv.shape[0]
        radius = (temp_bias.shape[-1] - 1) // 2
        my_index = lax.axis_index('frames')
        first_slots = (my_index * per_dev)[None]
        queue_len = groups * per_dev

        def one_step(current, noise_frame):
            x = jnp.einsum('fpc,cd->fpd', current.astype(jnp.bfloat16), w_in, preferred_element_type=jnp.float32)
            x = x.astype(jnp.bfloat16).astype(jnp.float32)
            for layer_id in range(layers):
                layer_mod = slot_mod[:, layer_id]
                x = spatial_block(x, layer_mod[:, 0], layer_mod[:, 1], spat_qkv[layer_id], spat_out[layer_id])
                u = modulate(x, layer_mod[:, 2], layer_mod[:, 3])
                heads_qkv = jnp.einsum('fpd,jdhe->jfphe', u, temp_qkv[layer_id], preferred_element_type=jnp.float32).astype(jnp.bfloat16)
                key_val = heads_qkv[1:]
                from_left = lax.ppermute(key_val[:, per_dev - radius:], 'frames', right_pairs)
                from_right = lax.ppermute(key_val[:, :radius], 'frames', left_pairs)
                extended = jnp.concatenate([from_left, key_val, from_right], axis=1)
                attended = temporal_attend(heads_qkv[0][None], extended[0][None], extended[1][None], temp_bias[layer_id], first_slots, 0, queue_len)
                x = x + jnp.einsum('fphe,hed->fpd', attended[0], temp_out[layer_id], preferred_element_type=jnp.float32)
                x = mlp_block(x, layer_mod[:, 4], layer_mod[:, 5], w_up[layer_id], w_down[layer_id])
            velocity = jnp.einsum('fpd,dc->fpc', x.astype(jnp.bfloat16), w_out, preferred_element_type=jnp.float32)
            updated = current + step_dt[:, None, None] * velocity
            arriving = lax.ppermute(updated[:1], 'frames', left_pairs)
            arriving = jnp.where(my_index == groups - 1, noise_frame[None], arriving)
            return jnp.concatenate([updated[1:], arriving], axis=0), updated[0]

        final_z, emitted = lax.scan(one_step, latents, new_noise)
        spread = lax.all_to_all(emitted, 'frames', 1, 0, tiled=True)
        return spread[:emitted.shape[0]], final_z

    return jax.shard_map(per_device, mesh=mesh, in_specs=(slot_spec, slot_spec, slot_spec, P('videos'), P(), P(), P(), P(), P(), P(), P(), P(), P()), out_specs=(P('videos', 'frames'), slot_spec), check_vma=False)
```

profile of v0, /device:TPU:97, one launch (start us, length us, event | category | flops | bytes accessed | tf_op | source)
XLA Modules:
  0.0 2213.5 jit_solution(15166452664383386138)
XLA Ops:
  9.1 2130.1 %while.16 = (s32[]{:T(128)}, f32[4,256,4]{1,2,0:T(4,128)S(1)}, f32[4,256,4]{1,2,0:T(4,128)}, f32[4]{0:T(128)}, bf16[4,384]{1,0:T(4,128)(2,1)}, /*index=5*/f32[4,...) while((s32[]{:T(128)}, f32[4,256,4]{1,2,0:T(4,128)S(1)}, ...), condition=%wide.region_61.62_spmd, body=%wide.region_0.61_spmd.sunk | while | flops 31791521792 | bytes 807128000 | solution.py:82
  39.6 13.4 collective-permute-done
  127.0 13.7 collective-permute-done.2
  145.8 10.2 copy.234
  213.4 13.7 collective-permute-done.4
  232.2 10.2 copy.237
  299.6 13.7 collective-permute-done.6
  385.9 13.7 collective-permute-done.8
  474.4 12.7 collective-permute-done.10
  492.1 10.2 copy.246
  570.5 13.5 collective-permute-done
  589.1 10.2 copy.231
  657.8 13.7 collective-permute-done.2
  676.6 10.2 copy.234
  744.2 13.7 collective-permute-done.4
  763.0 10.2 copy.237
  830.4 13.7 collective-permute-done.6
  916.7 13.7 collective-permute-done.8
  1005.2 12.7 collective-permute-done.10
  1101.3 13.5 collective-permute-done
  1188.6 13.7 collective-permute-done.2
  1275.0 13.7 collective-permute-done.4
  1361.2 13.7 collective-permute-done.6
  1447.5 13.7 collective-permute-done.8
  1535.9 12.7 collective-permute-done.10
  1635.2 13.5 collective-permute-done
  1722.6 13.7 collective-permute-done.2
  1808.9 13.7 collective-permute-done.4
  1895.2 13.7 collective-permute-done.6
  1981.8 13.7 collective-permute-done.8
  2070.2 12.7 collective-permute-done.10
  2140.8 69.0 %all_to_all.15 = f32[32,1,128]{2,1,0:T(1,128)S(1)} all-to-all(f32[32,1,128]{2,1,0:T(1,128)S(1)} %reshape.832), channel_id=1, replica_groups=mesh['videos'=1,'frames'=32] {'frames'}, dimensions={0} | all-to-all | bytes 32768 | tf_op jit(solution)/shard_map/all_to_all | solution.py:83
  (1038 shorter events, 1752.7 us)
Async XLA Ops:
  30.3 22.7 %collective-permute-start = (bf16[2,4,256,6,64]{2,4,3,0,1:T(8,128)(2,1)S(1)}, bf16[2,4,256,6,64]{2,4,3,0,1:T(8,128)(2,1)}, u32[]{:S(2)}, u32[]{:S(2)}) collective-permute-start(bf16[2,4,256,6,64]{2,4,3,0,1:T(8,128)(2,1)S(1)} %slice.1633), channel_id=1, source_target_pairs={{1,0},{2,1},{3,2},{4,3},{5,4},{6,5},{7,6},{8,7},{9,8},{10,9},{11,1... | collective-permute-start | bytes 4718600 | tf_op jit(solution)/shard_map/while/body/eval_jaxpr/ppermute | solution.py:71
  118.0 22.7 %collective-permute-start.2 = (bf16[2,4,256,6,64]{2,4,3,0,1:T(8,128)(2,1)S(1)}, bf16[2,4,256,6,64]{2,4,3,0,1:T(8,128)(2,1)}, u32[]{:S(2)}, u32[]{:S(2)}) collective-permute-start(bf16[2,4,256,6,64]{2,4,3,0,1:T(8,128)(2,1)S(1)} %slice.1634), channel_id=1, source_target_pairs={{1,0},{2,1},{3,2},{4,3},{5,4},{6,5},{7,6},{8,7},{9,8},{10,9},{11,1... | collective-permute-start | bytes 4718600 | tf_op jit(solution)/shard_map/while/body/eval_jaxpr/ppermute | solution.py:71
  120.1 21.8 collective-permute-start.3
  204.2 22.9 %collective-permute-start.4 = (bf16[2,4,256,6,64]{2,4,3,0,1:T(8,128)(2,1)S(1)}, bf16[2,4,256,6,64]{2,4,3,0,1:T(8,128)(2,1)}, u32[]{:S(2)}, u32[]{:S(2)}) collective-permute-start(bf16[2,4,256,6,64]{2,4,3,0,1:T(8,128)(2,1)S(1)} %slice.1635), channel_id=1, source_target_pairs={{1,0},{2,1},{3,2},{4,3},{5,4},{6,5},{7,6},{8,7},{9,8},{10,9},{11,1... | collective-permute-start | bytes 4718600 | tf_op jit(solution)/shard_map/while/body/eval_jaxpr/ppermute | solution.py:71
  206.5 21.8 collective-permute-start.5
  290.5 22.7 %collective-permute-start.6 = (bf16[2,4,256,6,64]{2,4,3,0,1:T(8,128)(2,1)S(1)}, bf16[2,4,256,6,64]{2,4,3,0,1:T(8,128)(2,1)}, u32[]{:S(2)}, u32[]{:S(2)}) collective-permute-start(bf16[2,4,256,6,64]{2,4,3,0,1:T(8,128)(2,1)S(1)} %slice.1636), channel_id=1, source_target_pairs={{1,0},{2,1},{3,2},{4,3},{5,4},{6,5},{7,6},{8,7},{9,8},{10,9},{11,1... | collective-permute-start | bytes 4718600 | tf_op jit(solution)/shard_map/while/body/eval_jaxpr/ppermute | solution.py:71
  376.9 22.7 %collective-permute-start.8 = (bf16[2,4,256,6,64]{2,4,3,0,1:T(8,128)(2,1)S(1)}, bf16[2,4,256,6,64]{2,4,3,0,1:T(8,128)(2,1)}, u32[]{:S(2)}, u32[]{:S(2)}) collective-permute-start(bf16[2,4,256,6,64]{2,4,3,0,1:T(8,128)(2,1)S(1)} %slice.1637), channel_id=1, source_target_pairs={{1,0},{2,1},{3,2},{4,3},{5,4},{6,5},{7,6},{8,7},{9,8},{10,9},{11,1... | collective-permute-start | bytes 4718600 | tf_op jit(solution)/shard_map/while/body/eval_jaxpr/ppermute | solution.py:71
  464.3 22.8 %collective-permute-start.10 = (bf16[2,4,256,6,64]{2,4,3,0,1:T(8,128)(2,1)S(1)}, bf16[2,4,256,6,64]{2,4,3,0,1:T(8,128)(2,1)}, u32[]{:S(2)}, u32[]{:S(2)}) collective-permute-start(bf16[2,4,256,6,64]{2,4,3,0,1:T(8,128)(2,1)S(1)} %slice.1638), channel_id=1, source_target_pairs={{1,0},{2,1},{3,2},{4,3},{5,4},{6,5},{7,6},{8,7},{9,8},{10,9},{11,1... | collective-permute-start | bytes 4718600 | tf_op jit(solution)/shard_map/while/body/eval_jaxpr/ppermute | solution.py:71
  562.3 21.8 collective-permute-start
  648.8 22.7 %collective-permute-start.2 = (bf16[2,4,256,6,64]{2,4,3,0,1:T(8,128)(2,1)S(1)}, bf16[2,4,256,6,64]{2,4,3,0,1:T(8,128)(2,1)}, u32[]{:S(2)}, u32[]{:S(2)}) collective-permute-start(bf16[2,4,256,6,64]{2,4,3,0,1:T(8,128)(2,1)S(1)} %slice.1634), channel_id=1, source_target_pairs={{1,0},{2,1},{3,2},{4,3},{5,4},{6,5},{7,6},{8,7},{9,8},{10,9},{11,1... | collective-permute-start | bytes 4718600 | tf_op jit(solution)/shard_map/while/body/eval_jaxpr/ppermute | solution.py:71
  734.9 22.9 %collective-permute-start.4 = (bf16[2,4,256,6,64]{2,4,3,0,1:T(8,128)(2,1)S(1)}, bf16[2,4,256,6,64]{2,4,3,0,1:T(8,128)(2,1)}, u32[]{:S(2)}, u32[]{:S(2)}) collective-permute-start(bf16[2,4,256,6,64]{2,4,3,0,1:T(8,128)(2,1)S(1)} %slice.1635), channel_id=1, source_target_pairs={{1,0},{2,1},{3,2},{4,3},{5,4},{6,5},{7,6},{8,7},{9,8},{10,9},{11,1... | collective-permute-start | bytes 4718600 | tf_op jit(solution)/shard_map/while/body/eval_jaxpr/ppermute | solution.py:71
  737.3 21.8 collective-permute-start.5
  821.3 22.7 %collective-permute-start.6 = (bf16[2,4,256,6,64]{2,4,3,0,1:T(8,128)(2,1)S(1)}, bf16[2,4,256,6,64]{2,4,3,0,1:T(8,128)(2,1)}, u32[]{:S(2)}, u32[]{:S(2)}) collective-permute-start(bf16[2,4,256,6,64]{2,4,3,0,1:T(8,128)(2,1)S(1)} %slice.1636), channel_id=1, source_target_pairs={{1,0},{2,1},{3,2},{4,3},{5,4},{6,5},{7,6},{8,7},{9,8},{10,9},{11,1... | collective-permute-start | bytes 4718600 | tf_op jit(solution)/shard_map/while/body/eval_jaxpr/ppermute | solution.py:71
  823.5 21.8 collective-permute-start.7
  907.7 22.7 %collective-permute-start.8 = (bf16[2,4,256,6,64]{2,4,3,0,1:T(8,128)(2,1)S(1)}, bf16[2,4,256,6,64]{2,4,3,0,1:T(8,128)(2,1)}, u32[]{:S(2)}, u32[]{:S(2)}) collective-permute-start(bf16[2,4,256,6,64]{2,4,3,0,1:T(8,128)(2,1)S(1)} %slice.1637), channel_id=1, source_target_pairs={{1,0},{2,1},{3,2},{4,3},{5,4},{6,5},{7,6},{8,7},{9,8},{10,9},{11,1... | collective-permute-start | bytes 4718600 | tf_op jit(solution)/shard_map/while/body/eval_jaxpr/ppermute | solution.py:71
  995.1 22.8 %collective-permute-start.10 = (bf16[2,4,256,6,64]{2,4,3,0,1:T(8,128)(2,1)S(1)}, bf16[2,4,256,6,64]{2,4,3,0,1:T(8,128)(2,1)}, u32[]{:S(2)}, u32[]{:S(2)}) collective-permute-start(bf16[2,4,256,6,64]{2,4,3,0,1:T(8,128)(2,1)S(1)} %slice.1638), channel_id=1, source_target_pairs={{1,0},{2,1},{3,2},{4,3},{5,4},{6,5},{7,6},{8,7},{9,8},{10,9},{11,1... | collective-permute-start | bytes 4718600 | tf_op jit(solution)/shard_map/while/body/eval_jaxpr/ppermute | solution.py:71
  1093.1 21.8 collective-permute-start
  1179.6 22.7 %collective-permute-start.2 = (bf16[2,4,256,6,64]{2,4,3,0,1:T(8,128)(2,1)S(1)}, bf16[2,4,256,6,64]{2,4,3,0,1:T(8,128)(2,1)}, u32[]{:S(2)}, u32[]{:S(2)}) collective-permute-start(bf16[2,4,256,6,64]{2,4,3,0,1:T(8,128)(2,1)S(1)} %slice.1634), channel_id=1, source_target_pairs={{1,0},{2,1},{3,2},{4,3},{5,4},{6,5},{7,6},{8,7},{9,8},{10,9},{11,1... | collective-permute-start | bytes 4718600 | tf_op jit(solution)/shard_map/while/body/eval_jaxpr/ppermute | solution.py:71
  1265.7 22.9 %collective-permute-start.4 = (bf16[2,4,256,6,64]{2,4,3,0,1:T(8,128)(2,1)S(1)}, bf16[2,4,256,6,64]{2,4,3,0,1:T(8,128)(2,1)}, u32[]{:S(2)}, u32[]{:S(2)}) collective-permute-start(bf16[2,4,256,6,64]{2,4,3,0,1:T(8,128)(2,1)S(1)} %slice.1635), channel_id=1, source_target_pairs={{1,0},{2,1},{3,2},{4,3},{5,4},{6,5},{7,6},{8,7},{9,8},{10,9},{11,1... | collective-permute-start | bytes 4718600 | tf_op jit(solution)/shard_map/while/body/eval_jaxpr/ppermute | solution.py:71
  1268.1 21.8 collective-permute-start.5
  1352.1 22.7 %collective-permute-start.6 = (bf16[2,4,256,6,64]{2,4,3,0,1:T(8,128)(2,1)S(1)}, bf16[2,4,256,6,64]{2,4,3,0,1:T(8,128)(2,1)}, u32[]{:S(2)}, u32[]{:S(2)}) collective-permute-start(bf16[2,4,256,6,64]{2,4,3,0,1:T(8,128)(2,1)S(1)} %slice.1636), channel_id=1, source_target_pairs={{1,0},{2,1},{3,2},{4,3},{5,4},{6,5},{7,6},{8,7},{9,8},{10,9},{11,1... | collective-permute-start | bytes 4718600 | tf_op jit(solution)/shard_map/while/body/eval_jaxpr/ppermute | solution.py:71
  1438.5 22.7 %collective-permute-start.8 = (bf16[2,4,256,6,64]{2,4,3,0,1:T(8,128)(2,1)S(1)}, bf16[2,4,256,6,64]{2,4,3,0,1:T(8,128)(2,1)}, u32[]{:S(2)}, u32[]{:S(2)}) collective-permute-start(bf16[2,4,256,6,64]{2,4,3,0,1:T(8,128)(2,1)S(1)} %slice.1637), channel_id=1, source_target_pairs={{1,0},{2,1},{3,2},{4,3},{5,4},{6,5},{7,6},{8,7},{9,8},{10,9},{11,1... | collective-permute-start | bytes 4718600 | tf_op jit(solution)/shard_map/while/body/eval_jaxpr/ppermute | solution.py:71
  1525.8 22.8 %collective-permute-start.10 = (bf16[2,4,256,6,64]{2,4,3,0,1:T(8,128)(2,1)S(1)}, bf16[2,4,256,6,64]{2,4,3,0,1:T(8,128)(2,1)}, u32[]{:S(2)}, u32[]{:S(2)}) collective-permute-start(bf16[2,4,256,6,64]{2,4,3,0,1:T(8,128)(2,1)S(1)} %slice.1638), channel_id=1, source_target_pairs={{1,0},{2,1},{3,2},{4,3},{5,4},{6,5},{7,6},{8,7},{9,8},{10,9},{11,1... | collective-permute-start | bytes 4718600 | tf_op jit(solution)/shard_map/while/body/eval_jaxpr/ppermute | solution.py:71
  1623.8 24.9 %collective-permute-start = (bf16[2,4,256,6,64]{2,4,3,0,1:T(8,128)(2,1)S(1)}, bf16[2,4,256,6,64]{2,4,3,0,1:T(8,128)(2,1)}, u32[]{:S(2)}, u32[]{:S(2)}) collective-permute-start(bf16[2,4,256,6,64]{2,4,3,0,1:T(8,128)(2,1)S(1)} %slice.1633), channel_id=1, source_target_pairs={{1,0},{2,1},{3,2},{4,3},{5,4},{6,5},{7,6},{8,7},{9,8},{10,9},{11,1... | collective-permute-start | bytes 4718600 | tf_op jit(solution)/shard_map/while/body/eval_jaxpr/ppermute | solution.py:71
  1625.8 24.1 %collective-permute-start.1 = (bf16[2,4,256,6,64]{2,4,3,0,1:T(8,128)(2,1)S(1)}, bf16[2,4,256,6,64]{2,4,3,0,1:T(8,128)(2,1)}, u32[]{:S(2)}, u32[]{:S(2)}) collective-permute-start(bf16[2,4,256,6,64]{2,4,3,0,1:T(8,128)(2,1)S(1)} %slice.1633), channel_id=1, source_target_pairs={{0,1},{1,2},{2,3},{3,4},{4,5},{5,6},{6,7},{7,8},{8,9},{9,10},{10,1... | collective-permute-start | bytes 4718600 | tf_op jit(solution)/shard_map/while/body/eval_jaxpr/ppermute | solution.py:70
  1713.5 22.7 %collective-permute-start.2 = (bf16[2,4,256,6,64]{2,4,3,0,1:T(8,128)(2,1)S(1)}, bf16[2,4,256,6,64]{2,4,3,0,1:T(8,128)(2,1)}, u32[]{:S(2)}, u32[]{:S(2)}) collective-permute-start(bf16[2,4,256,6,64]{2,4,3,0,1:T(8,128)(2,1)S(1)} %slice.1634), channel_id=1, source_target_pairs={{1,0},{2,1},{3,2},{4,3},{5,4},{6,5},{7,6},{8,7},{9,8},{10,9},{11,1... | collective-permute-start | bytes 4718600 | tf_op jit(solution)/shard_map/while/body/eval_jaxpr/ppermute | solution.py:71
  1799.7 22.9 %collective-permute-start.4 = (bf16[2,4,256,6,64]{2,4,3,0,1:T(8,128)(2,1)S(1)}, bf16[2,4,256,6,64]{2,4,3,0,1:T(8,128)(2,1)}, u32[]{:S(2)}, u32[]{:S(2)}) collective-permute-start(bf16[2,4,256,6,64]{2,4,3,0,1:T(8,128)(2,1)S(1)} %slice.1635), channel_id=1, source_target_pairs={{1,0},{2,1},{3,2},{4,3},{5,4},{6,5},{7,6},{8,7},{9,8},{10,9},{11,1... | collective-permute-start | bytes 4718600 | tf_op jit(solution)/shard_map/while/body/eval_jaxpr/ppermute | solution.py:71
  1802.1 21.8 collective-permute-start.5
  1886.1 22.7 %collective-permute-start.6 = (bf16[2,4,256,6,64]{2,4,3,0,1:T(8,128)(2,1)S(1)}, bf16[2,4,256,6,64]{2,4,3,0,1:T(8,128)(2,1)}, u32[]{:S(2)}, u32[]{:S(2)}) collective-permute-start(bf16[2,4,256,6,64]{2,4,3,0,1:T(8,128)(2,1)S(1)} %slice.1636), channel_id=1, source_target_pairs={{1,0},{2,1},{3,2},{4,3},{5,4},{6,5},{7,6},{8,7},{9,8},{10,9},{11,1... | collective-permute-start | bytes 4718600 | tf_op jit(solution)/shard_map/while/body/eval_jaxpr/ppermute | solution.py:71
  1972.5 23.0 %collective-permute-start.8 = (bf16[2,4,256,6,64]{2,4,3,0,1:T(8,128)(2,1)S(1)}, bf16[2,4,256,6,64]{2,4,3,0,1:T(8,128)(2,1)}, u32[]{:S(2)}, u32[]{:S(2)}) collective-permute-start(bf16[2,4,256,6,64]{2,4,3,0,1:T(8,128)(2,1)S(1)} %slice.1637), channel_id=1, source_target_pairs={{1,0},{2,1},{3,2},{4,3},{5,4},{6,5},{7,6},{8,7},{9,8},{10,9},{11,1... | collective-permute-start | bytes 4718600 | tf_op jit(solution)/shard_map/while/body/eval_jaxpr/ppermute | solution.py:71
  1974.6 22.1 collective-permute-start.9
  2060.1 22.8 %collective-permute-start.10 = (bf16[2,4,256,6,64]{2,4,3,0,1:T(8,128)(2,1)S(1)}, bf16[2,4,256,6,64]{2,4,3,0,1:T(8,128)(2,1)}, u32[]{:S(2)}, u32[]{:S(2)}) collective-permute-start(bf16[2,4,256,6,64]{2,4,3,0,1:T(8,128)(2,1)S(1)} %slice.1638), channel_id=1, source_target_pairs={{1,0},{2,1},{3,2},{4,3},{5,4},{6,5},{7,6},{8,7},{9,8},{10,9},{11,1... | collective-permute-start | bytes 4718600 | tf_op jit(solution)/shard_map/while/body/eval_jaxpr/ppermute | solution.py:71
  (157 other events, 2912.7 us)
where the time goes:
time: 2220 us; the launch traced here: 2210 us
  matrix products  755 us (34%)
  local copies, waits for them, and re-layouts  660 us (30%)
  waiting for transfers between devices  368 us (17%)
  other arithmetic  186 us (8%)
  starting transfers between devices  168 us (8%)
  blocking collectives  69 us (3%)
    another operation x120, local copies, waits for them, and re-layouts  578 us
    ppermute x24, waiting for transfers between devices, one_step(): from_right = lax.ppermute(key_val[:, :radius], 'frames', left_pairs)  324 us
    sub x24, matrix products, temporal_attend(): prob_mat = jax.nn.softmax(scores, axis=-1).astype(jnp.bfloat16)  195 us
    dot_general x24, matrix products, mlp_block(): jnp.einsum('fpm,md->fpd', hidden, down_l, preferred_element_type=jnp.floa...  126 us
    dot_general x24, matrix products, temporal_attend(): jnp.einsum('gphab,gbphe->gaphe', prob_mat, value_side, preferred_element_...  121 us
    dot_general x24, matrix products, spatial_block(): jnp.einsum('fphe,hed->fpd', attended, w_proj, preferred_element_type=jnp....  108 us
    ppermute x24, starting transfers between devices, one_step(): lax.ppermute(key_val[:, per_dev - radius:], 'frames', right_pairs)  107 us
    sub x24, other arithmetic, spatial_block(): jax.nn.softmax(scores * w_qkv.shape[-1] ** (-0.5), axis=-1)  102 us
  transfers between devices with their start and end apart: 52, of which 52 were waited for; matrix products, arithmetic and copies ran while one was open for 3% of the time, Pallas kernels for 0%

commit v1 on v0

v1 whole, which is shorter than its diff:
```python
import functools
import math

import jax
import jax.numpy as jnp
from jax import lax
from jax.experimental import pallas as pl
from jax.experimental.pallas import tpu as pltpu
from jax.sharding import PartitionSpec as P

F32 = jnp.float32
BF16 = jnp.bfloat16
NORM_EPS = 1e-6
LOG2E = math.log2(math.e)
MESH = pl.DeviceIdType.MESH
NEG = -1e30


def tdot(lhs, rhs):
    return lax.dot_general(lhs, rhs, (((0,), (0,)), ((), ())), preferred_element_type=F32)


def dot(lhs, rhs):
    return jnp.dot(lhs, rhs, preferred_element_type=F32)


def fold(op, x, rows=8):
    while x.shape[0] > rows and x.shape[0] % 2 == 0 and (x.shape[0] // 2) % 8 == 0:
        half = x.shape[0] // 2
        x = op(x[:half], x[half:])
    return x


def kernel(cfg, z_in, noise, mods, biasb, w_in, w_out, dt, sq_h, so_h, tq_h, to_h, up_h, dn_h,
           e_out, z_out,
           sq, so, tq, to, up, dn, wsem,
           x_ref, u_own, u_halo, send_sem, recv_sem,
           q_own, kv, qkv, o_ref, s_ref, p_ref, hid, part, pp,
           z_ref, z_snd, z_rcv, zsem, e_buf, e_send, e_recv):
    groups, layers, steps, per_dev, heads, radius = cfg
    d = x_ref.shape[1]
    tok = x_ref.shape[2]
    hd = d // heads
    wide = hid.shape[0]
    window = 2 * radius + 1
    lanes = 128
    chunks = tok // lanes
    scale = hd ** -0.5
    me = lax.axis_index('frames')
    left = lax.max(me - 1, 0)
    right = lax.min(me + 1, groups - 1)
    has_left = me > 0
    has_right = me < groups - 1

    pairs = ((sq_h, sq), (so_h, so), (tq_h, tq), (to_h, to), (up_h, up), (dn_h, dn))

    def wcopy(w, l):
        return pltpu.make_async_copy(pairs[w][0].at[l], pairs[w][1].at[l], wsem.at[w, l])

    def startw(l, _):
        for w in range(6):
            wcopy(w, l).start()
        return 0

    lax.fori_loop(0, layers, startw, 0)

    def u_copy(way, par, f):
        return pltpu.make_async_remote_copy(
            src_ref=u_own.at[f], dst_ref=u_halo.at[par, way, f],
            send_sem=send_sem.at[way, f], recv_sem=recv_sem.at[par, way, f],
            device_id={'frames': right if way == 0 else left}, device_id_type=MESH)

    def z_copy():
        return pltpu.make_async_remote_copy(
            src_ref=z_snd, dst_ref=z_rcv, send_sem=zsem.at[0], recv_sem=zsem.at[1],
            device_id={'frames': left}, device_id_type=MESH)

    def e_copy(s, t):
        return pltpu.make_async_remote_copy(
            src_ref=e_buf.at[s], dst_ref=e_buf.at[s], send_sem=e_send.at[s, t], recv_sem=e_recv.at[s],
            device_id={'frames': t}, device_id_type=MESH)

    z_ref[...] = jnp.zeros_like(z_ref)
    for f in range(per_dev):
        z_ref[f, 0:4, :] = z_in[f]
    part[...] = jnp.zeros_like(part)

    @pl.when(jnp.logical_not(has_left))
    def _():
        u_halo[:, 0] = jnp.zeros((2,) + u_halo.shape[2:], BF16)

    @pl.when(jnp.logical_not(has_right))
    def _():
        u_halo[:, 1] = jnp.zeros((2,) + u_halo.shape[2:], BF16)

    def modulated(f, l, first):
        x = x_ref[f]
        mean = jnp.sum(fold(jnp.add, x), axis=0, keepdims=True) * (1.0 / d)
        centred = x - mean
        var = jnp.sum(fold(jnp.add, centred * centred), axis=0, keepdims=True) * (1.0 / d)
        shift = mods[l, f, :, first:first + 1]
        gain = 1.0 + mods[l, f, :, first + 1:first + 2]
        return (centred * lax.rsqrt(var + NORM_EPS) * gain + shift).astype(BF16)

    def spatial(f, l):
        u = modulated(f, l, 0)
        qkv[...] = dot(sq[l], u).astype(BF16)
        for h in range(heads):
            q = qkv[h * hd:(h + 1) * hd, :]
            k = qkv[d + h * hd:d + (h + 1) * hd, :]
            s_ref[h] = tdot(k, q)
        for h in range(heads):
            s = s_ref[h]
            top = jnp.max(fold(jnp.maximum, s), axis=0, keepdims=True)
            e = jnp.exp2((s - top) * (scale * LOG2E))
            total = jnp.sum(fold(jnp.add, e), axis=0, keepdims=True)
            p_ref[h] = (e * (1.0 / total)).astype(BF16)
        for h in range(heads):
            v = qkv[2 * d + h * hd:2 * d + (h + 1) * hd, :]
            o_ref[h * hd:(h + 1) * hd, :] = dot(v, p_ref[h]).astype(BF16)
        x_ref[f] = x_ref[f] + tdot(so[l], o_ref[...])

    def project_temporal(f, l, par):
        u_own[f] = modulated(f, l, 2)
        r = dot(tq[l], u_own[f]).astype(BF16)
        q_own[f] = r[:d]
        kv[par, radius + f] = r[d:]

    def temporal(a, l, par):
        first = me * per_dev + a - radius
        for c in range(chunks):
            ln = slice(c * lanes, (c + 1) * lanes)
            for h in range(heads):
                qf = q_own[a, h * hd:(h + 1) * hd, ln].astype(F32)
                for j in range(window):
                    kf = kv[par, a + j, h * hd:(h + 1) * hd, ln].astype(F32)
                    part[j, c, h * 8:(h + 1) * 8, :] = fold(jnp.add, qf * kf)
            ss = []
            for j in range(window):
                s = part[j, c, pl.ds(0, 8, stride=8), :]
                for r in range(1, 8):
                    s = s + part[j, c, pl.ds(r, 8, stride=8), :]
                ok = (first + j >= 0) & (first + j < groups * per_dev)
                ss.append(jnp.where(ok, s * scale + biasb[l, j], NEG))
            top = functools.reduce(jnp.maximum, ss)
            es = [jnp.exp(s - top) for s in ss]
            inv = 1.0 / functools.reduce(jnp.add, es)
            for j in range(window):
                pp[j, c] = (es[j] * inv).astype(BF16).astype(F32)
        for c in range(chunks):
            ln = slice(c * lanes, (c + 1) * lanes)
            for h in range(heads):
                acc = None
                for j in range(window):
                    vf = kv[par, a + j, d + h * hd:d + (h + 1) * hd, ln].astype(F32)
                    pb = pp[j, c, pl.ds(h, 8, stride=0), :]
                    t = jnp.concatenate([pb] * (hd // 8), axis=0) * vf
                    acc = t if acc is None else acc + t
                o_ref[h * hd:(h + 1) * hd, ln] = acc.astype(BF16)
        x_ref[a] = x_ref[a] + tdot(to[l], o_ref[...])

    def mlp(a, l):
        u = modulated(a, l, 4)
        piece = d
        for c in range(wide // piece):
            h = tdot(up[l, :, c * piece:(c + 1) * piece], u)
            hid[c * piece:(c + 1) * piece, :] = jax.nn.gelu(h, approximate=True).astype(BF16)
        x_ref[a] = x_ref[a] + tdot(dn[l], hid[...])

    def body(it, _):
        lt = lax.rem(it + layers - 1, layers)
        ls = lax.rem(it, layers)
        step = lax.div(it - 1, layers)
        par = lax.rem(it, 2)
        run_t = it > 0
        run_s = it < steps * layers
        wrap = (ls == 0) & run_t

        @pl.when(it < layers)
        def _():
            for w in range(2):
                wcopy(w, ls).wait()
            wcopy(2, ls).wait()

        @pl.when(run_t & (it <= layers))
        def _():
            for w in range(3, 6):
                wcopy(w, lt).wait()

        @pl.when(run_t)
        def _():
            def halo(f, _):
                @pl.when(has_left)
                def _():
                    u_copy(0, 1 - par, f).wait_recv()

                @pl.when(has_right)
                def _():
                    u_copy(1, 1 - par, f).wait_recv()

                u2 = jnp.concatenate([u_halo[1 - par, 0, f], u_halo[1 - par, 1, f]], axis=1)
                r = dot(tq[lt, d:], u2).astype(BF16)
                kv[1 - par, f] = r[:, :tok]
                kv[1 - par, radius + per_dev + f] = r[:, tok:]
                return 0

            lax.fori_loop(0, per_dev, halo, 0)

        def frame(a, _):
            @pl.when(run_t & (a < per_dev))
            def _():
                temporal(a, lt, 1 - par)
                mlp(a, lt)

                @pl.when(has_right)
                def _():
                    u_copy(0, 1 - par, a).wait_send()

                @pl.when(has_left)
                def _():
                    u_copy(1, 1 - par, a).wait_send()

                @pl.when(ls == 0)
                def _():
                    v = dot(w_out[...], x_ref[a].astype(BF16))
                    new = z_ref[a] + dt[a] * v

                    @pl.when(a > 0)
                    def _():
                        z_ref[a - 1] = new

                    @pl.when((a == 0) & has_left)
                    def _():
                        z_snd[...] = new

                    @pl.when((a == 0) & jnp.logical_not(has_left))
                    def _():
                        e_buf[step] = new

            @pl.when(wrap & (a == 1) & has_left)
            def _():
                z_copy().start()

            @pl.when(wrap & (a == 1) & jnp.logical_not(has_left))
            def _():
                def snd(t, _):
                    e_copy(step, t).start()
                    return 0
                lax.fori_loop(1, groups, snd, 0)

            @pl.when(wrap & (a == per_dev))
            def _():
                @pl.when(has_right)
                def _():
                    z_copy().wait_recv()
                    z_ref[per_dev - 1] = z_rcv[...]

                @pl.when(jnp.logical_not(has_right))
                def _():
                    z_ref[per_dev - 1, 0:4, :] = noise[step]

                @pl.when(has_left)
                def _():
                    z_copy().wait_send()

            slot = lax.select(wrap, a - 1, a)

            @pl.when(run_s & (slot >= 0) & (slot < per_dev))
            def _():
                @pl.when(ls == 0)
                def _():
                    x_ref[slot] = tdot(w_in[...], z_ref[slot].astype(BF16)).astype(BF16).astype(F32)

                spatial(slot, ls)
                project_temporal(slot, ls, par)

                @pl.when(has_right)
                def _():
                    u_copy(0, par, slot).start()

                @pl.when(has_left)
                def _():
                    u_copy(1, par, slot).start()

            return 0

        lax.fori_loop(0, per_dev + 1, frame, 0)
        return 0

    lax.fori_loop(0, steps * layers + 1, body, 0)

    for f in range(per_dev):
        z_out[f] = z_ref[f, 0:4, :]

    @pl.when(has_left)
    def _():
        for s in range(steps):
            e_copy(s, 0).wait_recv()

    @pl.when(jnp.logical_not(has_left))
    def _():
        def fin(t, _):
            for s in range(steps):
                e_copy(s, t).wait_send()
            return 0
        lax.fori_loop(1, groups, fin, 0)

    e_out[...] = e_buf[...]


def solution(mesh):
    groups = mesh.shape['frames']
    slot_spec = P(('videos', 'frames'))

    def per_device(latents, slot_mod, step_dt, new_noise, w_in, spat_qkv, spat_out, temp_qkv, temp_out, temp_bias, w_up, w_down, w_out):
        per_dev, tok, ch = latents.shape
        layers, _, d, heads, hd = spat_qkv.shape
        steps = new_noise.shape[0]
        wide = w_up.shape[-1]
        window = temp_bias.shape[-1]
        radius = (window - 1) // 2

        z_t = jnp.swapaxes(latents, 1, 2)
        n_t = jnp.swapaxes(new_noise, 1, 2)
        mods = jnp.transpose(slot_mod, (1, 0, 3, 2))
        bias = jnp.pad(jnp.transpose(temp_bias, (0, 2, 1)), ((0, 0), (0, 0), (0, 8 - heads)))
        biasb = jnp.broadcast_to(bias[..., None], (layers, window, 8, 128))
        w_in8 = jnp.pad(w_in, ((0, 8 - ch), (0, 0)))
        w_out8 = jnp.pad(w_out.T, ((0, 8 - ch), (0, 0)))
        sq = jnp.transpose(spat_qkv, (0, 1, 3, 4, 2)).reshape(layers, 3 * d, d)
        tq = jnp.transpose(temp_qkv, (0, 1, 3, 4, 2)).reshape(layers, 3 * d, d)
        so = spat_out.reshape(layers, d, d)
        to = temp_out.reshape(layers, d, d)

        vm = pl.BlockSpec(memory_space=pltpu.VMEM)
        sm = pl.BlockSpec(memory_space=pltpu.SMEM)
        anys = pl.BlockSpec(memory_space=pl.ANY)
        V = pltpu.VMEM
        DMA = pltpu.SemaphoreType.DMA
        cfg = (groups, layers, steps, per_dev, heads, radius)
        e_all, z_fin = pl.pallas_call(
            functools.partial(kernel, cfg),
            out_shape=(jax.ShapeDtypeStruct((steps, 8, tok), F32), jax.ShapeDtypeStruct((per_dev, ch, tok), F32)),
            in_specs=[vm, vm, vm, vm, vm, vm, sm] + [anys] * 6,
            out_specs=(vm, vm),
            scratch_shapes=[
                V((layers, 3 * d, d), BF16), V((layers, d, d), BF16), V((layers, 3 * d, d), BF16), V((layers, d, d), BF16),
                V((layers, d, wide), BF16), V((layers, wide, d), BF16), DMA((6, layers)),
                V((per_dev, d, tok), F32), V((per_dev, d, tok), BF16), V((2, 2, per_dev, d, tok), BF16),
                DMA((2, per_dev)), DMA((2, 2, per_dev)),
                V((per_dev, d, tok), BF16), V((2, 2 * radius + per_dev, 2 * d, tok), BF16),
                V((3 * d, tok), BF16), V((d, tok), BF16),
                V((heads, tok, tok), F32), V((heads, tok, tok), BF16), V((wide, tok), BF16),
                V((window, tok // 128, 64, 128), F32), V((window, tok // 128, 8, 128), F32),
                V((per_dev, 8, tok), F32), V((8, tok), F32), V((8, tok), F32), DMA((2,)),
                V((steps, 8, tok), F32), DMA((steps, groups)), DMA((steps,)),
            ],
            compiler_params=pltpu.CompilerParams(has_side_effects=True, vmem_limit_bytes=64000000),
            name='fifo',
        )(z_t, n_t, mods, biasb, w_in8, w_out8, step_dt, sq, so, tq, to, w_up, w_down)

        me = lax.axis_index('frames')
        mine = tok // groups
        e_mine = lax.dynamic_slice_in_dim(e_all[:, :ch], me * mine, mine, 2)
        return jnp.swapaxes(e_mine, 1, 2), jnp.swapaxes(z_fin, 1, 2)

    return jax.shard_map(per_device, mesh=mesh, in_specs=(slot_spec, slot_spec, slot_spec, P('videos'), P(), P(), P(), P(), P(), P(), P(), P(), P()), out_specs=(P('videos', 'frames'), slot_spec), check_vma=False)
```

time: 2220 us -> 630 us (0.28)
  the two profiles are of different devices: /device:TPU:97 before, /device:TPU:103 now
where the time goes in v1:
time: 630 us
  Pallas kernels  619 us (98%)
  local copies, waits for them, and re-layouts  9.38 us (1%)
    pallas_call x1, Pallas kernels, per_device(): pl.pallas_call(functools.partial(kernel, cfg), out_shape=(jax.ShapeDtypeS...  619 us

profile of v1, /device:TPU:103, one launch (start us, length us, event | category | flops | bytes accessed | tf_op | source)
XLA Modules:
  0.0 629.5 jit_solution(5964989941055713049)
XLA Ops:
  0.6 0.0 copy-start
  0.6 0.0 copy-start.1
  0.7 3.7 copy.15
  4.4 0.9 copy.17
  5.3 0.8 broadcast_in_dim.2.biasb
  6.1 0.0 copy-done
  6.1 0.6 pad.12.w_in
  6.7 0.0 copy-done.1
  6.7 0.6 pad.13.w_out
  7.3 619.5 %fifo.1 = (f32[4,8,256]{2,1,0:T(8,128)}, f32[4,4,256]{2,1,0:T(4,128)}) custom-call(f32[4,4,256]{2,1,0:T(4,128)} %bitcast.22, f32[4,4,256]{2,1,0:T(4,128)} %bitcast.23, f32[6,4,384,6]{3,2,1,0:T(8,128)} %bitcast.16, f32[6,9,8,128]{3,2,1,0:T(8,128)} %broadcast_in_dim.2.biasb, bf16[8,384]{1,0:T(8,128)(2,1)} %pad.12.w_in, bf16[8,384]{1,0:T(8,128)(2,1)} %pad.13.w_out, ...), custom_call_target="tpu_custom_call" | custom-call | tf_op jit(solution)/shard_map/fifo/pallas_call | solution.py:341
  626.7 0.8 slice.3
  627.5 0.7 dynamic-slice_bitcast_fusion
  628.2 1.3 copy.19
  (1 shorter events, 0.0 us)
Async XLA Ops:
  0.6 5.4 copy-start
  0.6 6.0 copy-start.1
